TPU v7x, 32 devices: a whole 2x2x4 slice. The times are simulated.
32 devices in a mesh: ops: 8 (over z, y), site: 4 (over x, core).
Axes of the slice: x: 2, y: 2, z: 4, core: 2. Of those that a mesh axis runs over, the one named last changes fastest.
Arguments:
- wavefunction: bfloat16 [2048, 2048], replicated, may hold values from -6 to 6
- left_blocks: bfloat16 [64, 16, 192, 192], P('ops', 'site'), may hold values from -0.4375 to 0.4375
- right_blocks: bfloat16 [64, 16, 192, 192], P('ops', 'site'), may hold values from -0.15625 to 0.15625
- left_sector: int32 [2048], replicated, may hold values from 0 to 15, as said below
- right_sector: int32 [2048], replicated, may hold values from 0 to 15, as said below
- term_count: int32 [8], P('ops'), may hold values from 1 to 8, as said below
- left_energy: float32 [2048], replicated, may hold values from -1 to 1
- right_energy: float32 [2048], replicated, may hold values from -1 to 1
- subspace: bfloat16 [2, 16, 192, 2048], P(None, 'site'), may hold values from -0.0078125 to 0.0078125
Outputs:
- sigma: bfloat16 [16, 192, 2048], P('site')
- projections: float32 [2], replicated
Inputs may be any that keep to these rules, and one draw needn't show every extreme that they name: `left_sector`: sector ids never fall along the bond; each of the 16 sectors has 1 to 192 states and one has exactly 192. `right_sector`: sector ids never fall along the bond; each of the 16 sectors has 1 to 192 states and one has exactly 192. `term_count`: some group has all 8 slots live.
All inputs are finite; a program needn't handle non-finite values.
Results may differ from a plain program's by a relative error of at most 0.0045.
Values may be sent and summed in bfloat16 or wider, within the bound.
A program may use at most 192 MiB of HBM per device.

v0:
```python
import jax
import jax.numpy as jnp
from jax import lax
from jax.sharding import PartitionSpec as P


def sector_tables(sector_ids, sectors):
    labels = jnp.arange(sectors, dtype=jnp.int32)
    sector_starts = jnp.sum((sector_ids[None, :] < labels[:, None]).astype(jnp.int32), axis=1)
    sector_sizes = jnp.sum((sector_ids[None, :] == labels[:, None]).astype(jnp.int32), axis=1)
    return (sector_starts, sector_sizes)


def block_mask(size_now, widest):
    inside = jnp.arange(widest, dtype=jnp.int32) < size_now
    return inside[:, None] & inside[None, :]


def correlations(vectors, values):
    return jnp.sum(vectors.astype(jnp.float32) * values[None], axis=(1, 2, 3))


def local(
    wavefunction,
    left_blocks,
    right_blocks,
    left_sector,
    right_sector,
    term_count,
    left_energy,
    right_energy,
    subspace,
):
    slot_count = left_blocks.shape[0]
    sec_dev = left_blocks.shape[1]
    widest = left_blocks.shape[2]
    bond_dim = wavefunction.shape[0]
    row_count = sec_dev * widest
    sectors = sec_dev * lax.axis_size("site")
    left_start, left_size = sector_tables(left_sector, sectors)
    right_start, right_size = sector_tables(right_sector, sectors)
    active = term_count[0]
    first_sector = lax.axis_index("site") * sec_dev
    psi_padded = jnp.concatenate(
        [wavefunction, jnp.zeros((widest, bond_dim), wavefunction.dtype)], axis=0
    )
    energy_padded = jnp.concatenate([left_energy, jnp.zeros((widest,), jnp.float32)])
    psi_slabs = []
    energies = []
    left_masks = []
    inside_rows = []
    for within in range(sec_dev):
        sector = first_sector + within
        row_start = left_start[sector]
        size_now = left_size[sector]
        psi_slabs.append(lax.dynamic_slice_in_dim(psi_padded, row_start, widest, 0))
        energies.append(lax.dynamic_slice_in_dim(energy_padded, row_start, widest, 0))
        inside = jnp.arange(widest, dtype=jnp.int32) < size_now
        inside_rows.append(inside)
        left_masks.append(inside[:, None] & inside[None, :])

    def left_term(term_idx, stacked):
        blocks = lax.dynamic_index_in_dim(left_blocks, term_idx, 0, False)
        pieces = []
        for within in range(sec_dev):
            masked = jnp.where(left_masks[within], blocks[within], jnp.zeros((), blocks.dtype))
            pieces.append(jnp.dot(masked, psi_slabs[within], preferred_element_type=jnp.float32))
        left_image = jnp.concatenate(pieces, axis=0).astype(jnp.bfloat16)
        left_image = jnp.concatenate(
            [left_image, jnp.zeros((row_count, widest), jnp.bfloat16)], axis=1
        )
        return lax.dynamic_update_index_in_dim(stacked, left_image, term_idx, 0)

    images = lax.fori_loop(
        0, active, left_term, jnp.zeros((slot_count, row_count, bond_dim + widest), jnp.bfloat16)
    )
    part_blocks = lax.all_gather(right_blocks, "site", axis=1, tiled=True)

    def one_sector(within, summed):
        col_start = right_start[within]
        keep_mask = block_mask(right_size[within], widest)
        blocks = lax.dynamic_index_in_dim(part_blocks, within, 1, False)

        def add_term(term_idx, running):
            window = lax.dynamic_slice_in_dim(
                lax.dynamic_index_in_dim(images, term_idx, 0, False), col_start, widest, 1
            )
            one_block = jnp.where(
                keep_mask,
                lax.dynamic_index_in_dim(blocks, term_idx, 0, False),
                jnp.zeros((), blocks.dtype),
            )
            return running + lax.dot_general(
                window, one_block, (((1,), (1,)), ((), ())), preferred_element_type=jnp.float32
            )

        added = lax.fori_loop(0, active, add_term, jnp.zeros((row_count, widest), jnp.float32))
        previous = lax.dynamic_slice_in_dim(summed, col_start, widest, 1)
        return lax.dynamic_update_slice_in_dim(summed, previous + added, col_start, 1)

    folded = lax.fori_loop(
        0, part_blocks.shape[1], one_sector, jnp.zeros((row_count, bond_dim + widest), jnp.float32)
    )
    partial_value = folded[:, :bond_dim].reshape(sec_dev, widest, bond_dim)
    psi_mine = jnp.where(
        jnp.stack(inside_rows)[:, :, None],
        jnp.stack(psi_slabs).astype(jnp.float32),
        jnp.float32(0.0),
    )
    energy_mine = jnp.stack(energies)
    diagonal = (energy_mine[:, :, None] + right_energy[None, None, :]) * psi_mine
    col_width = bond_dim // lax.axis_size("ops")
    col_first = lax.axis_index("ops") * col_width
    col_share = lax.psum_scatter(
        partial_value, "ops", scatter_dimension=2, tiled=True
    ) + lax.dynamic_slice_in_dim(diagonal, col_first, col_width, 2)
    sigma_out = lax.all_gather(col_share.astype(jnp.bfloat16), "ops", axis=2, tiled=True)
    vectors_share = lax.dynamic_slice_in_dim(subspace, col_first, col_width, 3)
    projections = lax.psum(correlations(vectors_share, col_share), ("ops", "site"))
    return (sigma_out, projections)


def solution(mesh):
    in_specs = (
        P(),
        P("ops", "site", None, None),
        P("ops", "site", None, None),
        P(),
        P(),
        P("ops"),
        P(),
        P(),
        P(None, "site", None, None),
    )
    out_specs = (P("site", None, None), P())
    return jax.shard_map(local, mesh=mesh, in_specs=in_specs, out_specs=out_specs, check_vma=False)
```

profile of v0, /device:TPU:24, one launch (start us, length us, event | category | flops | bytes accessed | tf_op | source)
XLA Modules:
  0.0 753.4 jit_solution(12106594177710867749)
XLA Ops:
  7.2 3.9 copy.15
  21.9 5.4 pad_dynamic-slice_fusion
  27.4 9.5 %broadcast_in_dim.37 = bf16[8,768,2240]{2,1,0:T(8,128)(2,1)} broadcast(bf16[]{:T(256)} %constant.189.clone.1), dimensions={} | broadcast | bytes 27525122 | tf_op jit(solution)/shard_map/broadcast_in_dim | solution.py:75
  36.9 20.2 %while.63 = (s32[]{:T(128)}, bf16[8,768,2240]{2,1,0:T(8,128)(2,1)}, s32[]{:T(128)}, bf16[8,4,192,192]{3,2,1,0:T(8,128)(2,1)}, bf16[192,2048]{1,0:T(8,128)(2,1)},...) while((s32[]{:T(128)}, bf16[8,768,2240]{2,1,0:T(8,128)(2,1)}, ...), condition=%wide.region_5.6_spmd.clone, body=%wide.region_4.5_spmd.clone.sunk | while | flops 628211712 | bytes 13373707 | solution.py:74
  43.4 3.2 fusion.70
  53.1 3.3 fusion.70
  57.0 37.3 %all-gather.3.cloned.1.call-done = bf16[8,16,192,192]{3,2,0,1:T(8,128)(2,1)} async-done(((bf16[8,4,192,192]{3,2,0,1:T(8,128)(2,1)}), bf16[8,16,192,192]{3,2,0,1:T(8,128)(2,1)}) %all-gather.3.cloned.1.call-update) | async-done | bytes 9437200 | tf_op jit(solution)/shard_map/all_gather | solution.py:77
  94.3 3.3 broadcast_in_dim.32
  97.7 224.4 %while.62 = (s32[]{:T(128)}, f32[768,2240]{0,1:T(8,128)}, s32[16]{0:T(128)S(1)}, bf16[8,16,192,192]{3,2,0,1:T(8,128)(2,1)}, s32[16]{0:T(128)S(1)}, /*index=5*/s3...) while((s32[]{:T(128)}, f32[768,2240]{0,1:T(8,128)}, ...), condition=%wide.region_9.10_spmd, body=%wide.region_6.9_spmd.sunk | while | flops 56991944 | bytes 6391994 | solution.py:101
  102.7 4.9 while.64
  116.7 4.9 while.64
  130.7 4.9 while.64
  144.7 4.9 while.64
  158.8 4.9 while.64
  172.8 4.9 while.64
  186.8 4.9 while.64
  200.8 4.9 while.64
  214.9 4.9 while.64
  228.9 4.9 while.64
  242.9 4.9 while.64
  256.9 4.9 while.64
  263.0 3.0 dynamic_update_slice.19
  271.0 4.9 while.64
  285.0 4.9 while.64
  299.0 4.9 while.64
  313.0 4.9 while.64
  322.1 5.8 slice.19
  327.9 6.6 copy.16
  338.3 339.3 %reduce-scatter.2.cloned.1.call-done = f32[4,192,256]{2,1,0:T(8,128)} async-done(((f32[4,192,2048]{2,1,0:T(8,128)}), f32[4,192,256]{2,1,0:T(8,128)}) %reduce-scatter.2.cloned.1.call-update) | async-done | bytes 786448 | tf_op jit(solution)/shard_map/reduce_scatter | solution.py:114
  681.7 41.4 %psum.7 = f32[2]{0:T(128)} all-reduce(f32[2]{0:T(128)S(1)} %multiply_reduce_fusion), channel_id=1, replica_groups=mesh['ops'=8,'site'=4] {'ops','site'}, use_global_device_ids=true, to_apply=%region_12.13 | all-reduce | flops 2 | bytes 16 | tf_op jit(solution)/shard_map/psum | solution.py:119
  723.1 19.8 %all-gather.5.cloned.1.call-done = bf16[4,192,2048]{2,1,0:T(8,128)(2,1)} async-done(((bf16[4,192,256]{2,1,0:T(8,128)(2,1)}), bf16[4,192,2048]{2,1,0:T(8,128)(2,1)}) %all-gather.5.cloned.1.call-update) | async-done | bytes 3145744 | tf_op jit(solution)/shard_map/all_gather | solution.py:117
  742.9 4.0 copy.38
  (184 shorter events, 180.9 us)
Async XLA Ops:
  7.2 4.0 copy-start.3
  7.2 14.6 %copy-start.4 = (s32[2048]{0:T(1024)S(1)}, s32[2048]{0:T(1024)}, u32[]{:S(2)}) copy-start(s32[2048]{0:T(1024)} %param.19) | copy-start | bytes 24580
  7.2 87.2 %all-gather.3.cloned.1.call-start = ((), (), s32[]{:S(2)}) async-start(), calls=%async_computation.1 | async-start | bytes 15728640 | tf_op jit(solution)/shard_map/all_gather | solution.py:77
  11.1 666.5 %reduce-scatter.2.cloned.1.call-start = ((), (), s32[]{:S(2)}) async-start(), calls=%async_computation.2 | async-start | bytes 7077888 | tf_op jit(solution)/shard_map/reduce_scatter | solution.py:114
  334.5 3.6 copy-start.2
  334.5 343.1 %copy-start = (bf16[192,2048]{1,0:T(8,128)(2,1)S(1)}, bf16[192,2048]{1,0:T(8,128)(2,1)}, u32[]{:S(2)}) copy-start(bf16[192,2048]{1,0:T(8,128)(2,1)} %get-tuple-element.839) | copy-start | bytes 2359300
  334.5 343.1 %copy-start.1 = (bf16[192,2048]{1,0:T(8,128)(2,1)S(1)}, bf16[192,2048]{1,0:T(8,128)(2,1)}, u32[]{:S(2)}) copy-start(bf16[192,2048]{1,0:T(8,128)(2,1)} %get-tuple-element.840) | copy-start | bytes 2359300
  334.6 408.3 %all-gather.5.cloned.1.call-start = ((), (), s32[]{:S(2)}) async-start(), calls=%async_computation.3 | async-start | bytes 3538944 | tf_op jit(solution)/shard_map/all_gather | solution.py:117
Sparse Core Ops, SparseCore 0:
  11.3 83.0 all-gather.2
  334.7 342.8 reduce-scatter.1
  680.2 62.6 all-gather.4
where the time goes:
time: 768 us; the launch traced here: 753 us
  waiting for transfers between devices  397 us (52%)
  local copies, waits for them, and re-layouts  126 us (16%)
  loops' own time  65.7 us (9%)
  matrix products  57.9 us (8%)
  other arithmetic  44.9 us (6%)
  blocking collectives  41.4 us (5%)
  between operations  21 us (3%)
    reduce_scatter x1, waiting for transfers between devices, local(): lax.psum_scatter(partial_value, 'ops', scatter_dimension=2, tiled=True)  339 us
    dynamic_update_slice x16, local copies, waits for them, and re-layouts, one_sector(): lax.dynamic_update_slice_in_dim(summed, previous + added, col_start, 1)  47.2 us
    dot_general x32, matrix products, add_term(): lax.dot_general(window, one_block, (((1,), (1,)), ((), ())), preferred_el...  46.3 us
    psum x1, blocking collectives, local(): lax.psum(correlations(vectors_share, col_share), ('ops', 'site'))  41.4 us
    all_gather x1, waiting for transfers between devices, local(): part_blocks = lax.all_gather(right_blocks, 'site', axis=1, tiled=True)  37.3 us
    another operation x16, loops' own time, one_sector(): lax.fori_loop(0, active, add_term, jnp.zeros((row_count, widest), jnp.flo...  32 us
    another operation x1, loops' own time, local(): lax.fori_loop(0, part_blocks.shape[1], one_sector, jnp.zeros((row_count,...  31.6 us
    all_gather x1, waiting for transfers between devices, local(): lax.all_gather(col_share.astype(jnp.bfloat16), 'ops', axis=2, tiled=True)  19.8 us
  transfers between devices with their start and end apart: 3, of which 3 were waited for; matrix products, arithmetic and copies ran while one was open for 6% of the time, Pallas kernels for 0%

commit v1 on v0

v1 whole, which is shorter than its diff:
```python
import functools

import jax
import jax.numpy as jnp
from jax import lax
from jax.experimental import pallas as pl
from jax.experimental.pallas import tpu as pltpu
from jax.sharding import PartitionSpec as P

LANE = 128
MESH = pl.DeviceIdType.MESH


def sector_tables(sector_ids, sectors):
    labels = jnp.arange(sectors, dtype=jnp.int32)
    sector_starts = jnp.sum((sector_ids[None, :] < labels[:, None]).astype(jnp.int32), axis=1)
    sector_sizes = jnp.sum((sector_ids[None, :] == labels[:, None]).astype(jnp.int32), axis=1)
    return (sector_starts, sector_sizes)


def round_up(value, step):
    return (value + step - 1) // step * step


def apply_kernel(
    slots, sec_dev, widest, wide, window,
    starts, sizes, left_ref, slab_ref, right_ref, vectors_ref,
    part_ref, corr_ref,
    psi_pad, images, right_pad, summed,
):
    step = pl.program_id(0)
    rows = sec_dev * widest
    bond_dim = part_ref.shape[1]

    @pl.when(step == 0)
    def _():
        summed[...] = jnp.zeros_like(summed)
        right_pad[...] = jnp.zeros_like(right_pad)

    start = starts[step]
    size_now = sizes[step]
    first = pl.multiple_of(start // LANE * LANE, LANE)
    offset = start - first
    place = lax.broadcasted_iota(jnp.int32, (window, wide), 0)
    column = lax.broadcasted_iota(jnp.int32, (window, wide), 1)
    pick = ((place == column + offset) & (column < size_now)).astype(jnp.bfloat16)
    psi_pad[...] = jnp.dot(
        slab_ref[:, pl.ds(first, window)], pick, preferred_element_type=jnp.float32
    ).astype(jnp.bfloat16)
    for slot in range(slots):
        right_pad[0:widest, slot * wide : slot * wide + widest] = right_ref[slot, 0]
    for within in range(sec_dev):
        at = within * widest
        image = jnp.dot(
            left_ref[within], psi_pad[at : at + widest, :], preferred_element_type=jnp.float32
        ).astype(jnp.bfloat16)
        for slot in range(slots):
            images[at : at + widest, slot * wide : (slot + 1) * wide] = image[
                slot * widest : (slot + 1) * widest, :
            ]
    added = lax.dot_general(
        images[...], right_pad[...], (((1,), (1,)), ((), ())), preferred_element_type=jnp.float32
    )
    high = added.astype(jnp.bfloat16)
    low = (added - high.astype(jnp.float32)).astype(jnp.bfloat16)
    back = (((1,), (1,)), ((), ()))
    summed[:, pl.ds(first, window)] += lax.dot_general(
        high, pick, back, preferred_element_type=jnp.float32
    ) + lax.dot_general(low, pick, back, preferred_element_type=jnp.float32)

    @pl.when(step == pl.num_programs(0) - 1)
    def _():
        chunk = 16
        vectors = vectors_ref.shape[0]

        def fold(idx, totals):
            at = pl.multiple_of(idx * chunk, chunk)
            values = summed[pl.ds(at, chunk), 0:bond_dim]
            part_ref[pl.ds(at, chunk), :] = values.astype(jnp.bfloat16)
            new = []
            for k in range(vectors):
                product = vectors_ref[k, pl.ds(at, chunk), :].astype(jnp.float32) * values
                folded = product[0:8] + product[8:16]
                pieces = [folded[:, c : c + LANE] for c in range(0, bond_dim, LANE)]
                while len(pieces) > 1:
                    pieces = [a + b for a, b in zip(pieces[0::2], pieces[1::2])]
                new.append(totals[k] + pieces[0])
            return tuple(new)

        totals = lax.fori_loop(
            0, rows // chunk, fold, tuple(jnp.zeros((8, LANE), jnp.float32) for _ in range(vectors))
        )
        for k in range(vectors):
            corr_ref[k] = totals[k]


def exchange_kernel(
    groups, sites,
    part_ref, psi_ref, left_e_ref, right_e_ref, corr_ref,
    out_ref, corr_out,
    pair_in, sending, outer_in, corr_ops, corr_sites,
    pair_s, pair_r, outer_s, outer_r, gath_s, gath_r, fwd_s, fwd_r, ops_s, ops_r, site_s, site_r,
):
    outer = groups // 2
    me = lax.axis_index("ops")
    here = lax.axis_index("site")
    row = me // 2
    side = me % 2
    peer = row * 2 + 1 - side
    rows, bond_dim = part_ref.shape[1], part_ref.shape[2]
    step = 256

    barrier = pltpu.get_barrier_semaphore()
    for k in range(1, groups):
        pl.semaphore_signal(
            barrier, inc=1, device_id={"ops": lax.rem(me + k, groups)}, device_id_type=MESH
        )
    for k in range(1, sites):
        pl.semaphore_signal(
            barrier, inc=1, device_id={"site": lax.rem(here + k, sites)}, device_id_type=MESH
        )
    pl.semaphore_wait(barrier, groups - 1 + sites - 1)

    def remote(src, dst, send_sem, recv_sem, target):
        return pltpu.make_async_remote_copy(
            src_ref=src, dst_ref=dst, send_sem=send_sem, recv_sem=recv_sem,
            device_id=target, device_id_type=MESH,
        )

    pair = []
    for k in range(outer):
        dest = lax.rem(row + k + 1, outer)
        copy = remote(
            part_ref.at[dest * 2 + 1 - side], pair_in.at[k], pair_s.at[k], pair_r.at[k], {"ops": peer}
        )
        copy.start()
        pair.append(copy)

    corr_copies = []
    for k in range(1, groups):
        copy = remote(
            corr_ref, corr_ops.at[k], ops_s.at[k], ops_r.at[k], {"ops": lax.rem(me + k, groups)}
        )
        copy.start()
        corr_copies.append(copy)
    corr_ops[0] = corr_ref[...]

    sends = []
    for k in range(outer - 1):
        dest = lax.rem(row + k + 1, outer)
        mine = dest * 2 + side
        pair[k].wait_recv()

        def add(c, carry, k=k, mine=mine):
            cols = pl.ds(pl.multiple_of(c * step, step), step)
            sending[k, :, cols] = (
                part_ref[mine, :, cols].astype(jnp.float32) + pair_in[k, :, cols].astype(jnp.float32)
            ).astype(jnp.bfloat16)
            return carry

        lax.fori_loop(0, bond_dim // step, add, 0)
        copy = remote(sending.at[k], outer_in.at[k], outer_s.at[k], outer_r.at[k], {"ops": mine})
        copy.start()
        sends.append(copy)

    pair[outer - 1].wait_recv()
    for copy in sends:
        copy.wait_recv()

    def finish(c, carry):
        cols = pl.ds(pl.multiple_of(c * step, step), step)
        total = part_ref[me, :, cols].astype(jnp.float32) + pair_in[outer - 1, :, cols].astype(
            jnp.float32
        )
        for k in range(outer - 1):
            total = total + outer_in[k, :, cols].astype(jnp.float32)
        total = total + (left_e_ref[...] + right_e_ref[:, cols]) * psi_ref[:, cols].astype(jnp.float32)
        out_ref[me, :, cols] = total.astype(jnp.bfloat16)
        return carry

    lax.fori_loop(0, bond_dim // step, finish, 0)

    gathers = []
    for k in range(outer - 1):
        dest = lax.rem(row + k + 1, outer)
        copy = remote(
            out_ref.at[me], out_ref.at[me], gath_s.at[k], gath_r.at[k], {"ops": dest * 2 + side}
        )
        copy.start()
        gathers.append(copy)
    forwards = [remote(out_ref.at[me], out_ref.at[me], fwd_s.at[outer - 1], fwd_r.at[outer - 1], {"ops": peer})]
    forwards[0].start()

    for copy in corr_copies:
        copy.wait_recv()

    def corr_add(g, total):
        return total + corr_ops[lax.rem(me - g + groups, groups)]

    corr_sites[0] = lax.fori_loop(0, groups, corr_add, jnp.zeros(corr_ref.shape, jnp.float32))
    site_copies = []
    for k in range(1, sites):
        copy = remote(
            corr_sites.at[0], corr_sites.at[k], site_s.at[k], site_r.at[k],
            {"site": lax.rem(here + k, sites)},
        )
        copy.start()
        site_copies.append(copy)

    for k in range(outer - 1):
        source = lax.rem(row - k - 1 + outer, outer)
        slot = source * 2 + side
        remote(
            out_ref.at[slot], out_ref.at[slot], gath_s.at[k], gath_r.at[k], {"ops": peer}
        ).wait_recv()
        copy = remote(out_ref.at[slot], out_ref.at[slot], fwd_s.at[k], fwd_r.at[k], {"ops": peer})
        copy.start()
        forwards.append(copy)

    for copy in site_copies:
        copy.wait_recv()

    def site_add(g, total):
        return total + corr_sites[lax.rem(here - g + sites, sites)]

    corr_out[...] = lax.fori_loop(0, sites, site_add, jnp.zeros(corr_ref.shape, jnp.float32))

    remote(
        out_ref.at[peer], out_ref.at[peer], fwd_s.at[outer - 1], fwd_r.at[outer - 1], {"ops": peer}
    ).wait_recv()
    for k in range(outer - 1):
        source = lax.rem(row - k - 1 + outer, outer)
        slot = source * 2 + 1 - side
        remote(out_ref.at[slot], out_ref.at[slot], fwd_s.at[k], fwd_r.at[k], {"ops": peer}).wait_recv()
    for copy in pair + corr_copies + sends + gathers + forwards + site_copies:
        copy.wait_send()


def local(
    wavefunction,
    left_blocks,
    right_blocks,
    left_sector,
    right_sector,
    term_count,
    left_energy,
    right_energy,
    subspace,
):
    slots, sec_dev, widest = left_blocks.shape[0], left_blocks.shape[1], left_blocks.shape[2]
    bond_dim = wavefunction.shape[0]
    vectors = subspace.shape[0]
    rows = sec_dev * widest
    sites = lax.axis_size("site")
    groups = lax.axis_size("ops")
    sectors = sec_dev * sites
    wide = round_up(widest, 256)
    window = round_up(widest + LANE - 1, LANE)
    padded_cols = round_up(bond_dim, LANE) - LANE + window

    gathered = lax.all_gather(right_blocks, "site", axis=1, tiled=True)

    left_start, left_size = sector_tables(left_sector, sectors)
    right_start, right_size = sector_tables(right_sector, sectors)
    first_sector = lax.axis_index("site") * sec_dev
    psi_padded = jnp.pad(wavefunction, ((0, widest), (0, padded_cols - bond_dim)))
    energy_padded = jnp.pad(left_energy, (0, widest))
    slabs = []
    energies = []
    insides = []
    for within in range(sec_dev):
        row_start = left_start[first_sector + within]
        inside = jnp.arange(widest, dtype=jnp.int32) < left_size[first_sector + within]
        slab = lax.dynamic_slice_in_dim(psi_padded, row_start, widest, 0)
        slabs.append(jnp.where(inside[:, None], slab, jnp.zeros((), slab.dtype)))
        energies.append(lax.dynamic_slice_in_dim(energy_padded, row_start, widest, 0))
        insides.append(inside)
    slab = jnp.concatenate(slabs, axis=0)
    energy = jnp.concatenate(energies)
    inside = jnp.stack(insides)
    live = jnp.arange(slots, dtype=jnp.int32) < term_count[0]
    keep = live[:, None, None, None] & inside[None, :, :, None] & inside[None, :, None, :]
    left = jnp.where(keep, left_blocks, jnp.zeros((), left_blocks.dtype))
    left = left.transpose(1, 0, 2, 3).reshape(sec_dev, slots * widest, widest)
    vectors_flat = subspace.reshape(vectors, rows, bond_dim)

    own = lax.axis_index("ops")
    psi_mine = slab[:, :bond_dim]
    diagonal = (energy[:, None] + right_energy[None, :]) * psi_mine.astype(jnp.float32)
    first_group = jnp.where(own == 0, jnp.float32(1.0), jnp.float32(0.0))
    corr_diag = first_group * jnp.sum(
        vectors_flat.astype(jnp.float32) * diagonal[None], axis=(1, 2)
    )

    vmem = pl.BlockSpec(memory_space=pltpu.VMEM)
    smem = pl.BlockSpec(memory_space=pltpu.SMEM)
    part, corr = pl.pallas_call(
        functools.partial(apply_kernel, slots, sec_dev, widest, wide, window),
        grid=(sectors,),
        out_shape=(
            jax.ShapeDtypeStruct((rows, bond_dim), jnp.bfloat16),
            jax.ShapeDtypeStruct((vectors, 8, LANE), jnp.float32),
        ),
        in_specs=[
            smem,
            smem,
            vmem,
            vmem,
            pl.BlockSpec((slots, 1, widest, widest), lambda step: (0, step, 0, 0)),
            vmem,
        ],
        out_specs=(vmem, vmem),
        scratch_shapes=[
            pltpu.VMEM((rows, wide), jnp.bfloat16),
            pltpu.VMEM((rows, slots * wide), jnp.bfloat16),
            pltpu.VMEM((wide, slots * wide), jnp.bfloat16),
            pltpu.VMEM((rows, padded_cols), jnp.float32),
        ],
        compiler_params=pltpu.CompilerParams(
            dimension_semantics=("arbitrary",), vmem_limit_bytes=60 * 1024 * 1024
        ),
        name="apply_terms",
    )(right_start, right_size, left, slab, gathered, vectors_flat)

    share = rows // groups
    corr_mine = jnp.sum(corr, axis=(1, 2)) + corr_diag
    corr_tile = jnp.broadcast_to(corr_mine[:, None, None], (vectors, 8, LANE))
    psi_share = lax.dynamic_slice_in_dim(psi_mine, own * share, share, 0)
    energy_share = lax.dynamic_slice_in_dim(energy, own * share, share, 0)[:, None]
    outer = groups // 2
    dma = pltpu.SemaphoreType.DMA
    sigma, corr_all = pl.pallas_call(
        functools.partial(exchange_kernel, groups, sites),
        out_shape=(
            jax.ShapeDtypeStruct((groups, share, bond_dim), jnp.bfloat16),
            jax.ShapeDtypeStruct((vectors, 8, LANE), jnp.float32),
        ),
        in_specs=[vmem] * 5,
        out_specs=(vmem, vmem),
        scratch_shapes=[
            pltpu.VMEM((outer, share, bond_dim), jnp.bfloat16),
            pltpu.VMEM((max(outer - 1, 1), share, bond_dim), jnp.bfloat16),
            pltpu.VMEM((max(outer - 1, 1), share, bond_dim), jnp.bfloat16),
            pltpu.VMEM((groups, vectors, 8, LANE), jnp.float32),
            pltpu.VMEM((sites, vectors, 8, LANE), jnp.float32),
            dma((outer,)), dma((outer,)),
            dma((outer,)), dma((outer,)),
            dma((outer,)), dma((outer,)),
            dma((outer,)), dma((outer,)),
            dma((groups,)), dma((groups,)),
            dma((sites,)), dma((sites,)),
        ],
        compiler_params=pltpu.CompilerParams(
            collective_id=0, has_side_effects=True, vmem_limit_bytes=60 * 1024 * 1024
        ),
        name="exchange_rows",
    )(
        part.reshape(groups, share, bond_dim),
        psi_share,
        energy_share,
        right_energy[None, :],
        corr_tile,
    )
    return (sigma.reshape(sec_dev, widest, bond_dim), corr_all[:, 0, 0])


def solution(mesh):
    in_specs = (
        P(),
        P("ops", "site", None, None),
        P("ops", "site", None, None),
        P(),
        P(),
        P("ops"),
        P(),
        P(),
        P(None, "site", None, None),
    )
    out_specs = (P("site", None, None), P())
    return jax.shard_map(local, mesh=mesh, in_specs=in_specs, out_specs=out_specs, check_vma=False)
```

time: 768 us -> 287 us (0.37); the launches traced: 753 us -> 287 us
  waiting for transfers between devices: 397 us -> 49.3 us
  Pallas kernels: 0 us -> 180 us
  local copies, waits for them, and re-layouts: 126 us -> 13.7 us
  loops' own time: 65.7 us -> 0 us
  matrix products: 57.9 us -> 0 us
  blocking collectives: 41.4 us -> 0 us
  other arithmetic: 44.9 us -> 20.7 us
    reduce_scatter x1 -> x0, waiting for transfers between devices: 339 us -> none  [local(): lax.psum_scatter(partial_value, 'ops', scatter_dimension=2, tiled=True)]
    pallas_call x0 -> x2, Pallas kernels: none -> 180 us  [the longest x1 107 us: local(): pl.pallas_call(functools.partial(exchange_kernel, groups, sites), out_sha...]
    another operation x18 -> x0, loops' own time: 65.7 us -> none  [the longest x16 32 us: one_sector(): lax.fori_loop(0, active, add_term, jnp.zeros((row_count, widest), jnp.flo...]
    dot_general x40 -> x0, matrix products: 57.9 us -> none  [the longest x32 46.3 us: add_term(): lax.dot_general(window, one_block, (((1,), (1,)), ((), ())), preferred_el...]
    dynamic_update_slice x16 -> x0, local copies, waits for them, and re-layouts: 47.2 us -> none  [one_sector(): lax.dynamic_update_slice_in_dim(summed, previous + added, col_start, 1)]
    psum x1 -> x0, blocking collectives: 41.4 us -> none  [local(): lax.psum(correlations(vectors_share, col_share), ('ops', 'site'))]
    dynamic_slice x35 -> x2, local copies, waits for them, and re-layouts: 25.7 us -> 2.46 us  [the longest x1 1.77 us: local(): psi_share = lax.dynamic_slice_in_dim(psi_mine, own * share, share, 0)]
    squeeze x16 -> x0, local copies, waits for them, and re-layouts: 19.1 us -> none  [one_sector(): blocks = lax.dynamic_index_in_dim(part_blocks, within, 1, False)]
  transfers between devices with their start and end apart: 3 -> 1, of which waited for: 3 -> 1; matrix products, arithmetic and copies ran while one was open for 6% -> 10% of each run, Pallas kernels for 0% -> 0%
where the time goes in v1:
time: 287 us
  Pallas kernels  180 us (63%)
  waiting for transfers between devices  49.3 us (17%)
  between operations  22.5 us (8%)
  other arithmetic  20.7 us (7%)
  local copies, waits for them, and re-layouts  13.7 us (5%)
    pallas_call x1, Pallas kernels, local(): pl.pallas_call(functools.partial(exchange_kernel, groups, sites), out_sha...  107 us
    pallas_call x1, Pallas kernels, local(): pl.pallas_call(functools.partial(apply_kernel, slots, sec_dev, widest, wi...  73.4 us
    all_gather x1, waiting for transfers between devices, local(): gathered = lax.all_gather(right_blocks, 'site', axis=1, tiled=True)  48.6 us
  transfers between devices with their start and end apart: 1, of which 1 were waited for; matrix products, arithmetic and copies ran while one was open for 10% of the time, Pallas kernels for 0%

profile of v1, /device:TPU:24, one launch (start us, length us, event | category | flops | bytes accessed | tf_op | source)
XLA Modules:
  0.0 286.5 jit_solution(5808914761725336029)
XLA Ops:
  7.2 0.7 all-gather.2.cloned.1.call-update
  7.9 0.8 convert_reduce_fusion
  8.7 0.7 fusion.5
  15.2 0.6 iota_compare_fusion.8
  15.8 0.6 iota_compare_fusion.9
  16.5 0.7 iota_compare_fusion.10
  17.2 0.6 iota_compare_fusion.11
  17.7 0.1 broadcast_and_fusion
  17.8 3.7 %fusion = bf16[4,8,192,192]{3,2,0,1:T(8,128)(2,1)S(1)} fusion(bf16[8,4,192,192]{3,2,1,0:T(8,128)(2,1)} %param.10, pred[4,192]{1,0:T(4,128)(4,1)S(1)} %pad_add_fusion, pred[8,4,192]{2,1,0:T(4,128)(4,1)S(1)} %broadcast_and_fusion), kind=kLoop, calls=%fused_computation.8 | loop fusion | flops 2359296 | bytes 4725504 | tf_op jit(solution)/shard_map/transpose | solution.py:284
  21.5 2.0 copy.15
  26.1 0.6 iota_compare_fusion.7
  26.6 0.7 iota_compare_fusion.6
  27.3 0.6 iota_compare_fusion.5
  28.0 0.6 iota_compare_fusion.4
  28.6 3.2 %fusion.1 = (bf16[192,2304]{1,0:T(8,128)(2,1)S(1)}, bf16[192,2304]{1,0:T(8,128)(2,1)S(1)}, bf16[192,2304]{1,0:T(8,128)(2,1)S(1)}, bf16[192,2304]{1,0:T(8,128)(2,1)S(1)}) fusion(s32[]{:T(128)S(6)} %select_n.62, bf16[2048,2048]{1,0:T(8,128)(2,1)} %param.9, pred[192]{0:T(512)(128)(4,1)S(1)} %iota_compare_fusion.7, s32[]{:T(128)S(6)} %select_n.64, ...), kind=kLoop, calls=%fused_computation.9 | loop fusion | flops 1769472 | bytes 11928336 | tf_op jit(solution)/shard_map/jit(_where)/select_n | solution.py:275
  31.8 0.3 pad_maximum_fusion.slab_ref
  32.1 2.4 slice.8
  34.5 0.1 pad_dynamic-slice_fusion.7
  34.6 0.1 pad_maximum_fusion.1
  34.7 0.1 dynamic-slice_bitcast_fusion
  34.8 0.7 copy.16.left_e_ref
  35.5 1.3 convert_reduce_fusion.2
  36.9 1.8 constant_dynamic-slice_fusion.psi_ref
  38.6 0.7 convert_multiply_fusion
  39.3 4.7 %multiply_reduce_fusion = f32[2]{0:T(128)S(1)} fusion(bf16[2,4,192,2048]{3,2,1,0:T(8,128)(2,1)} %param.17, f32[4,192,2048]{2,1,0:T(8,128)S(1)} %bitcast.20), kind=kLoop, calls=%fused_computation | loop fusion | flops 9437182 | bytes 12582920 | tf_op jit(solution)/shard_map/reduce_sum | solution.py:291
  44.0 48.6 %all-gather.2.cloned.1.call-done.right_ref = bf16[8,16,192,192]{3,2,1,0:T(8,128)(2,1)} async-done(((bf16[8,4,192,192]{3,2,1,0:T(8,128)(2,1)}), bf16[8,16,192,192]{3,2,1,0:T(8,128)(2,1)}) %all-gather.2.cloned.1.call-update) | async-done | bytes 9437200 | tf_op jit(solution)/shard_map/all_gather | solution.py:261
  92.6 73.4 %apply_terms.1 = (bf16[768,2048]{1,0:T(8,128)(2,1)}, f32[2,8,128]{2,1,0:T(8,128)}) custom-call(s32[16]{0:T(128)} %get-tuple-element.13.starts, s32[16]{0:T(128)} %get-tuple-element.12.sizes, bf16[4,1536,192]{2,1,0:T(8,128)(2,1)} %bitcast.22, bf16[768,2304]{1,0:T(8,128)(2,1)} %copy-done, bf16[8,16,192,192]{3,2,1,0:T(8,128)(2,1)} %all-gather.2.cloned.1.call-done.right_ref, ...), custom_call_target="tpu_custom_call" | custom-call | tf_op jit(solution)/shard_map/apply_terms/pallas_call | solution.py:297
  166.0 0.8 reduce_sum.58
  166.8 0.7 broadcast_in_dim.72.corr_ref
  167.5 106.9 %exchange_rows.1 = (bf16[8,96,2048]{2,1,0:T(8,128)(2,1)}, f32[2,8,128]{2,1,0:T(8,128)}) custom-call(bf16[8,96,2048]{2,1,0:T(8,128)(2,1)} %bitcast.23, bf16[96,2048]{1,0:T(8,128)(2,1)} %constant_dynamic-slice_fusion.psi_ref, f32[96,1]{1,0:T(8,128)} %copy.16.left_e_ref, f32[1,2048]{1,0:T(1,128)} %bitcast.25, f32[2,8,128]{2,1,0:T(8,128)} %broadcast_in_dim.72.corr_ref), custom_call_target="tpu_custom_call" | custom-call | tf_op jit(solution)/shard_map/exchange_rows/pallas_call | solution.py:332
  274.4 1.3 slice_reduce_fusion
  275.7 4.0 %copy.19 = bf16[4,192,2048]{2,1,0:T(8,128)(2,1)} copy(bf16[4,192,2048]{2,1,0:T(8,128)(2,1)} %bitcast.24) | data formatting | bytes 6291456
  (10 shorter events, 0.1 us)
Async XLA Ops:
  7.2 85.5 %all-gather.2.cloned.1.call-start = ((), (), s32[]{:S(2)}) async-start(), calls=%async_computation | async-start | bytes 15728640 | tf_op jit(solution)/shard_map/all_gather | solution.py:261
  31.8 2.8 copy-start.2
  31.8 6.8 %copy-start.1 = (f32[2048]{0:T(1024)S(1)}, f32[2048]{0:T(1024)}, u32[]{:S(2)}) copy-start(f32[2048]{0:T(1024)} %param.16) | copy-start | bytes 24580
  32.1 7.2 %copy-start = (bf16[768,2304]{1,0:T(8,128)(2,1)}, bf16[768,2304]{1,0:T(8,128)(2,1)S(1)}, u32[]{:S(2)}) copy-start(bf16[768,2304]{1,0:T(8,128)(2,1)S(1)} %pad_maximum_fusion.slab_ref) | copy-start | bytes 10616836
Sparse Core Ops, SparseCore 0:
  9.5 83.0 all-gather.1

commit v2 on v1

--- a/solution.py
+++ b/solution.py
@@ -23,20 +23,137 @@
 
 
 def apply_kernel(
-    slots, sec_dev, widest, wide, window,
-    starts, sizes, left_ref, slab_ref, right_ref, vectors_ref,
-    part_ref, corr_ref,
-    psi_pad, images, right_pad, summed,
+    slots, sec_dev, widest, wide,
+    left_ref, spread_ref, right_ref,
+    out_ref,
+    psi_pad, images, right_pad, arrived, added,
+    pair_s, pair_r, outer_s, outer_r, fwd_s, fwd_r, out_s,
 ):
+    me = lax.axis_index("site")
+    row = me // 2
+    side = me % 2
+    peer = row * 2 + 1 - side
+    across = (1 - row) * 2 + side
+    far = (1 - row) * 2 + 1 - side
+    pairs = slots // 2
+    shift = wide - widest
+
+    barrier = pltpu.get_barrier_semaphore()
+    for other in (peer, across):
+        pl.semaphore_signal(barrier, inc=1, device_id={"site": other}, device_id_type=MESH)
+    pl.semaphore_wait(barrier, 2)
+
+    def to_pair(w):
+        return pltpu.make_async_remote_copy(
+            src_ref=right_ref.at[w], dst_ref=arrived.at[0, w], send_sem=pair_s.at[w],
+            recv_sem=pair_r.at[w], device_id={"site": peer}, device_id_type=MESH,
+        )
+
+    def to_across(w):
+        return pltpu.make_async_remote_copy(
+            src_ref=right_ref.at[w], dst_ref=arrived.at[1, w], send_sem=outer_s.at[w],
+            recv_sem=outer_r.at[w], device_id={"site": across}, device_id_type=MESH,
+        )
+
+    def forward(w):
+        return pltpu.make_async_remote_copy(
+            src_ref=arrived.at[1, w], dst_ref=arrived.at[2, w], send_sem=fwd_s.at[w],
+            recv_sem=fwd_r.at[w], device_id={"site": peer}, device_id_type=MESH,
+        )
+
+    for w in range(sec_dev):
+        to_across(w).start()
+    for w in range(sec_dev):
+        to_pair(w).start()
+    right_pad[...] = jnp.zeros_like(right_pad)
+    lane_in = lax.broadcasted_iota(jnp.int32, (wide, wide), 0)
+    lane_out = lax.broadcasted_iota(jnp.int32, (wide, wide), 1)
+    moved = (lane_in + shift == lane_out).astype(jnp.bfloat16)
+
+    def keep(slot, sector):
+        return pltpu.make_async_copy(added.at[slot], out_ref.at[sector], out_s.at[slot])
+
+    def one_sector(i, carry):
+        @pl.when((i % 3 == 0) & (i > 0) & (i <= 3 * sec_dev))
+        def _():
+            w = i // 3 - 1
+            to_across(w).wait_recv()
+            forward(w).start()
+
+        @pl.when(i < sec_dev)
+        def _():
+            right_pad[0:widest, :] = right_ref[jnp.minimum(i, sec_dev - 1)]
+
+        @pl.when((i >= sec_dev) & (i < 2 * sec_dev))
+        def _():
+            w = jnp.clip(i - sec_dev, 0, sec_dev - 1)
+            to_pair(w).wait_recv()
+            right_pad[0:widest, :] = arrived[0, w]
+
+        later = jnp.maximum(i - 2 * sec_dev, 0)
+        late_w = later // 2
+
+        @pl.when((i >= 2 * sec_dev) & (i % 2 == 0))
+        def _():
+            right_pad[0:widest, :] = arrived[1, late_w]
+
+        @pl.when((i >= 2 * sec_dev) & (i % 2 == 1))
+        def _():
+            forward(late_w).wait_recv()
+            right_pad[0:widest, :] = arrived[2, late_w]
+
+        early = i < 2 * sec_dev
+        owner = jnp.where(
+            early,
+            jnp.where(i < sec_dev, me, peer),
+            jnp.where(i % 2 == 0, across, far),
+        )
+        sector = owner * sec_dev + jnp.where(early, i % sec_dev, late_w)
+        psi_pad[0] = spread_ref[sector]
+        psi_pad[1] = jnp.dot(
+            spread_ref[sector], moved, preferred_element_type=jnp.float32
+        ).astype(jnp.bfloat16)
+        for within in range(sec_dev):
+            at = within * widest
+            even, odd = (
+                jnp.dot(
+                    left_ref[within, parity],
+                    psi_pad[parity, at : at + widest, :],
+                    preferred_element_type=jnp.float32,
+                ).astype(jnp.bfloat16)
+                for parity in range(2)
+            )
+            for p in range(pairs):
+                rows = slice(p * widest, (p + 1) * widest)
+                base = 2 * p * widest
+                images[at : at + widest, base : base + LANE] = even[rows, :LANE]
+                images[at : at + widest, base + LANE : base + 2 * LANE] = (
+                    even[rows, LANE:] + odd[rows, :LANE]
+                )
+                images[at : at + widest, base + 2 * LANE : base + 3 * LANE] = odd[rows, LANE:]
+        slot = i % 2
+
+        @pl.when(i >= 2)
+        def _():
+            keep(slot, sector).wait()
+
+        added[slot] = lax.dot_general(
+            images[...], right_pad[...], (((1,), (1,)), ((), ())), preferred_element_type=jnp.float32
+        )
+        keep(slot, sector).start()
+        return carry
+
+    lax.fori_loop(0, 4 * sec_dev, one_sector, 0)
+    for slot in range(2):
+        keep(slot, 0).wait()
+    for w in range(sec_dev):
+        to_pair(w).wait_send()
+        to_across(w).wait_send()
+        forward(w).wait_send()
+
+
+def spread_kernel(wide, window, starts, sizes, slab_ref, spread_ref):
     step = pl.program_id(0)
-    rows = sec_dev * widest
-    bond_dim = part_ref.shape[1]
-
-    @pl.when(step == 0)
-    def _():
-        summed[...] = jnp.zeros_like(summed)
-        right_pad[...] = jnp.zeros_like(right_pad)
-
     start = starts[step]
     size_now = sizes[step]
     first = pl.multiple_of(start // LANE * LANE, LANE)
@@ -44,23 +161,29 @@
     place = lax.broadcasted_iota(jnp.int32, (window, wide), 0)
     column = lax.broadcasted_iota(jnp.int32, (window, wide), 1)
     pick = ((place == column + offset) & (column < size_now)).astype(jnp.bfloat16)
-    psi_pad[...] = jnp.dot(
+    spread_ref[0] = jnp.dot(
         slab_ref[:, pl.ds(first, window)], pick, preferred_element_type=jnp.float32
     ).astype(jnp.bfloat16)
-    for slot in range(slots):
-        right_pad[0:widest, slot * wide : slot * wide + widest] = right_ref[slot, 0]
-    for within in range(sec_dev):
-        at = within * widest
-        image = jnp.dot(
-            left_ref[within], psi_pad[at : at + widest, :], preferred_element_type=jnp.float32
-        ).astype(jnp.bfloat16)
-        for slot in range(slots):
-            images[at : at + widest, slot * wide : (slot + 1) * wide] = image[
-                slot * widest : (slot + 1) * widest, :
-            ]
-    added = lax.dot_general(
-        images[...], right_pad[...], (((1,), (1,)), ((), ())), preferred_element_type=jnp.float32
-    )
+
+
+def place_kernel(
+    widest, wide, window, starts, sizes, added_ref, vectors_ref, part_ref, corr_ref, summed
+):
+    step = pl.program_id(0)
+    rows, bond_dim = part_ref.shape
+
+    @pl.when(step == 0)
+    def _():
+        summed[...] = jnp.zeros_like(summed)
+
+    start = starts[step]
+    size_now = sizes[step]
+    first = pl.multiple_of(start // LANE * LANE, LANE)
+    offset = start - first
+    place = lax.broadcasted_iota(jnp.int32, (window, wide), 0)
+    column = lax.broadcasted_iota(jnp.int32, (window, wide), 1)
+    pick = ((place == column + offset) & (column < size_now)).astype(jnp.bfloat16)
+    added = added_ref[0]
     high = added.astype(jnp.bfloat16)
     low = (added - high.astype(jnp.float32)).astype(jnp.bfloat16)
     back = (((1,), (1,)), ((), ()))
@@ -127,14 +250,20 @@
             device_id=target, device_id_type=MESH,
         )
 
+    halves = 2
+    width = bond_dim // halves
+    parts = [pl.ds(h * width, width) for h in range(halves)]
+
     pair = []
-    for k in range(outer):
-        dest = lax.rem(row + k + 1, outer)
-        copy = remote(
-            part_ref.at[dest * 2 + 1 - side], pair_in.at[k], pair_s.at[k], pair_r.at[k], {"ops": peer}
-        )
-        copy.start()
-        pair.append(copy)
+    for h in range(halves):
+        for k in range(outer):
+            dest = lax.rem(row + k + 1, outer)
+            copy = remote(
+                part_ref.at[dest * 2 + 1 - side, :, parts[h]], pair_in.at[k, :, parts[h]],
+                pair_s.at[h, k], pair_r.at[h, k], {"ops": peer},
+            )
+            copy.start()
+            pair.append(copy)
 
     corr_copies = []
     for k in range(1, groups):
@@ -146,50 +275,62 @@
     corr_ops[0] = corr_ref[...]
 
     sends = []
-    for k in range(outer - 1):
-        dest = lax.rem(row + k + 1, outer)
-        mine = dest * 2 + side
-        pair[k].wait_recv()
-
-        def add(c, carry, k=k, mine=mine):
-            cols = pl.ds(pl.multiple_of(c * step, step), step)
-            sending[k, :, cols] = (
-                part_ref[mine, :, cols].astype(jnp.float32) + pair_in[k, :, cols].astype(jnp.float32)
-            ).astype(jnp.bfloat16)
+    for h in range(halves):
+        for k in range(outer - 1):
+            dest = lax.rem(row + k + 1, outer)
+            mine = dest * 2 + side
+            pair[h * outer + k].wait_recv()
+
+            def add(c, carry, k=k, mine=mine, h=h):
+                cols = pl.ds(pl.multiple_of(h * width + c * step, step), step)
+                sending[k, :, cols] = (
+                    part_ref[mine, :, cols].astype(jnp.float32)
+                    + pair_in[k, :, cols].astype(jnp.float32)
+                ).astype(jnp.bfloat16)
+                return carry
+
+            lax.fori_loop(0, width // step, add, 0)
+            copy = remote(
+                sending.at[k, :, parts[h]], outer_in.at[k, :, parts[h]],
+                outer_s.at[h, k], outer_r.at[h, k], {"ops": mine},
+            )
+            copy.start()
+            sends.append(copy)
+
+    gathers = []
+    forwards = []
+    for h in range(halves):
+        pair[h * outer + outer - 1].wait_recv()
+        for copy in sends[h * (outer - 1) : (h + 1) * (outer - 1)]:
+            copy.wait_recv()
+
+        def finish(c, carry, h=h):
+            cols = pl.ds(pl.multiple_of(h * width + c * step, step), step)
+            total = part_ref[me, :, cols].astype(jnp.float32) + pair_in[
+                outer - 1, :, cols
+            ].astype(jnp.float32)
+            for k in range(outer - 1):
+                total = total + outer_in[k, :, cols].astype(jnp.float32)
+            total = total + (left_e_ref[...] + right_e_ref[:, cols]) * psi_ref[:, cols].astype(
+                jnp.float32
+            )
+            out_ref[me, :, cols] = total.astype(jnp.bfloat16)
             return carry
 
-        lax.fori_loop(0, bond_dim // step, add, 0)
-        copy = remote(sending.at[k], outer_in.at[k], outer_s.at[k], outer_r.at[k], {"ops": mine})
+        lax.fori_loop(0, width // step, finish, 0)
+        block = out_ref.at[me, :, parts[h]]
+        for k in range(outer - 1):
+            dest = lax.rem(row + k + 1, outer)
+            copy = remote(
+                block, block, gath_s.at[h, k], gath_r.at[h, k], {"ops": dest * 2 + side}
+            )
+            copy.start()
+            gathers.append(copy)
+        copy = remote(
+            block, block, fwd_s.at[h, outer - 1], fwd_r.at[h, outer - 1], {"ops": peer}
+        )
         copy.start()
-        sends.append(copy)
-
-    pair[outer - 1].wait_recv()
-    for copy in sends:
-        copy.wait_recv()
-
-    def finish(c, carry):
-        cols = pl.ds(pl.multiple_of(c * step, step), step)
-        total = part_ref[me, :, cols].astype(jnp.float32) + pair_in[outer - 1, :, cols].astype(
-            jnp.float32
-        )
-        for k in range(outer - 1):
-            total = total + outer_in[k, :, cols].astype(jnp.float32)
-        total = total + (left_e_ref[...] + right_e_ref[:, cols]) * psi_ref[:, cols].astype(jnp.float32)
-        out_ref[me, :, cols] = total.astype(jnp.bfloat16)
-        return carry
-
-    lax.fori_loop(0, bond_dim // step, finish, 0)
-
-    gathers = []
-    for k in range(outer - 1):
-        dest = lax.rem(row + k + 1, outer)
-        copy = remote(
-            out_ref.at[me], out_ref.at[me], gath_s.at[k], gath_r.at[k], {"ops": dest * 2 + side}
-        )
-        copy.start()
-        gathers.append(copy)
-    forwards = [remote(out_ref.at[me], out_ref.at[me], fwd_s.at[outer - 1], fwd_r.at[outer - 1], {"ops": peer})]
-    forwards[0].start()
+        forwards.append(copy)
 
     for copy in corr_copies:
         copy.wait_recv()
@@ -207,15 +348,14 @@
         copy.start()
         site_copies.append(copy)
 
-    for k in range(outer - 1):
-        source = lax.rem(row - k - 1 + outer, outer)
-        slot = source * 2 + side
-        remote(
-            out_ref.at[slot], out_ref.at[slot], gath_s.at[k], gath_r.at[k], {"ops": peer}
-        ).wait_recv()
-        copy = remote(out_ref.at[slot], out_ref.at[slot], fwd_s.at[k], fwd_r.at[k], {"ops": peer})
-        copy.start()
-        forwards.append(copy)
+    for h in range(halves):
+        for k in range(outer - 1):
+            source = lax.rem(row - k - 1 + outer, outer)
+            block = out_ref.at[source * 2 + side, :, parts[h]]
+            remote(block, block, gath_s.at[h, k], gath_r.at[h, k], {"ops": peer}).wait_recv()
+            copy = remote(block, block, fwd_s.at[h, k], fwd_r.at[h, k], {"ops": peer})
+            copy.start()
+            forwards.append(copy)
 
     for copy in site_copies:
         copy.wait_recv()
@@ -225,13 +365,15 @@
 
     corr_out[...] = lax.fori_loop(0, sites, site_add, jnp.zeros(corr_ref.shape, jnp.float32))
 
-    remote(
-        out_ref.at[peer], out_ref.at[peer], fwd_s.at[outer - 1], fwd_r.at[outer - 1], {"ops": peer}
-    ).wait_recv()
-    for k in range(outer - 1):
-        source = lax.rem(row - k - 1 + outer, outer)
-        slot = source * 2 + 1 - side
-        remote(out_ref.at[slot], out_ref.at[slot], fwd_s.at[k], fwd_r.at[k], {"ops": peer}).wait_recv()
+    for h in range(halves):
+        block = out_ref.at[peer, :, parts[h]]
+        remote(
+            block, block, fwd_s.at[h, outer - 1], fwd_r.at[h, outer - 1], {"ops": peer}
+        ).wait_recv()
+        for k in range(outer - 1):
+            source = lax.rem(row - k - 1 + outer, outer)
+            block = out_ref.at[source * 2 + 1 - side, :, parts[h]]
+            remote(block, block, fwd_s.at[h, k], fwd_r.at[h, k], {"ops": peer}).wait_recv()
     for copy in pair + corr_copies + sends + gathers + forwards + site_copies:
         copy.wait_send()
 
@@ -258,7 +400,8 @@
     window = round_up(widest + LANE - 1, LANE)
     padded_cols = round_up(bond_dim, LANE) - LANE + window
 
-    gathered = lax.all_gather(right_blocks, "site", axis=1, tiled=True)
+    assert sites == 4 and slots % 2 == 0 and 2 * (wide - widest) == LANE and wide == 2 * LANE
+    right = right_blocks.transpose(1, 2, 0, 3).reshape(sec_dev, widest, slots * widest)
 
     left_start, left_size = sector_tables(left_sector, sectors)
     right_start, right_size = sector_tables(right_sector, sectors)
@@ -281,7 +424,8 @@
     live = jnp.arange(slots, dtype=jnp.int32) < term_count[0]
     keep = live[:, None, None, None] & inside[None, :, :, None] & inside[None, :, None, :]
     left = jnp.where(keep, left_blocks, jnp.zeros((), left_blocks.dtype))
-    left = left.transpose(1, 0, 2, 3).reshape(sec_dev, slots * widest, widest)
+    left = left.reshape(slots // 2, 2, sec_dev, widest, widest).transpose(2, 1, 0, 3, 4)
+    left = left.reshape(sec_dev, 2, slots // 2 * widest, widest)
     vectors_flat = subspace.reshape(vectors, rows, bond_dim)
 
     own = lax.axis_index("ops")
@@ -294,33 +438,54 @@
 
     vmem = pl.BlockSpec(memory_space=pltpu.VMEM)
     smem = pl.BlockSpec(memory_space=pltpu.SMEM)
+    dma = pltpu.SemaphoreType.DMA
+    spread = pl.pallas_call(
+        functools.partial(spread_kernel, wide, window),
+        grid=(sectors,),
+        out_shape=jax.ShapeDtypeStruct((sectors, rows, wide), jnp.bfloat16),
+        in_specs=[smem, smem, vmem],
+        out_specs=pl.BlockSpec((1, rows, wide), lambda step: (step, 0, 0)),
+        compiler_params=pltpu.CompilerParams(
+            dimension_semantics=("arbitrary",), vmem_limit_bytes=40 * 1024 * 1024
+        ),
+        name="spread_columns",
+    )(right_start, right_size, slab)
+    added = pl.pallas_call(
+        functools.partial(apply_kernel, slots, sec_dev, widest, wide),
+        out_shape=jax.ShapeDtypeStruct((sectors, rows, wide), jnp.float32),
+        in_specs=[vmem, vmem, vmem],
+        out_specs=pl.BlockSpec(memory_space=pl.ANY),
+        scratch_shapes=[
+            pltpu.VMEM((2, rows, wide), jnp.bfloat16),
+            pltpu.VMEM((rows, slots * widest), jnp.bfloat16),
+            pltpu.VMEM((wide, slots * widest), jnp.bfloat16),
+            pltpu.VMEM((3, sec_dev, widest, slots * widest), jnp.bfloat16),
+            pltpu.VMEM((2, rows, wide), jnp.float32),
+            dma((sec_dev,)), dma((sec_dev,)),
+            dma((sec_dev,)), dma((sec_dev,)),
+            dma((sec_dev,)), dma((sec_dev,)),
+            dma((2,)),
+        ],
+        compiler_params=pltpu.CompilerParams(
+            collective_id=1, has_side_effects=True, vmem_limit_bytes=60 * 1024 * 1024
+        ),
+        name="apply_terms",
+    )(left, spread, right)
     part, corr = pl.pallas_call(
-        functools.partial(apply_kernel, slots, sec_dev, widest, wide, window),
+        functools.partial(place_kernel, widest, wide, window),
         grid=(sectors,),
         out_shape=(
             jax.ShapeDtypeStruct((rows, bond_dim), jnp.bfloat16),
             jax.ShapeDtypeStruct((vectors, 8, LANE), jnp.float32),
         ),
-        in_specs=[
-            smem,
-            smem,
-            vmem,
-            vmem,
-            pl.BlockSpec((slots, 1, widest, widest), lambda step: (0, step, 0, 0)),
-            vmem,
-        ],
+        in_specs=[smem, smem, pl.BlockSpec((1, rows, wide), lambda step: (step, 0, 0)), vmem],
         out_specs=(vmem, vmem),
-        scratch_shapes=[
-            pltpu.VMEM((rows, wide), jnp.bfloat16),
-            pltpu.VMEM((rows, slots * wide), jnp.bfloat16),
-            pltpu.VMEM((wide, slots * wide), jnp.bfloat16),
-            pltpu.VMEM((rows, padded_cols), jnp.float32),
-        ],
+        scratch_shapes=[pltpu.VMEM((rows, padded_cols), jnp.float32)],
         compiler_params=pltpu.CompilerParams(
             dimension_semantics=("arbitrary",), vmem_limit_bytes=60 * 1024 * 1024
         ),
-        name="apply_terms",
-    )(right_start, right_size, left, slab, gathered, vectors_flat)
+        name="place_columns",
+    )(right_start, right_size, added, vectors_flat)
 
     share = rows // groups
     corr_mine = jnp.sum(corr, axis=(1, 2)) + corr_diag
@@ -328,7 +493,6 @@
     psi_share = lax.dynamic_slice_in_dim(psi_mine, own * share, share, 0)
     energy_share = lax.dynamic_slice_in_dim(energy, own * share, share, 0)[:, None]
     outer = groups // 2
-    dma = pltpu.SemaphoreType.DMA
     sigma, corr_all = pl.pallas_call(
         functools.partial(exchange_kernel, groups, sites),
         out_shape=(
@@ -343,10 +507,10 @@
             pltpu.VMEM((max(outer - 1, 1), share, bond_dim), jnp.bfloat16),
             pltpu.VMEM((groups, vectors, 8, LANE), jnp.float32),
             pltpu.VMEM((sites, vectors, 8, LANE), jnp.float32),
-            dma((outer,)), dma((outer,)),
-            dma((outer,)), dma((outer,)),
-            dma((outer,)), dma((outer,)),
-            dma((outer,)), dma((outer,)),
+            dma((2, outer)), dma((2, outer)),
+            dma((2, outer)), dma((2, outer)),
+            dma((2, outer)), dma((2, outer)),
+            dma((2, outer)), dma((2, outer)),
             dma((groups,)), dma((groups,)),
             dma((sites,)), dma((sites,)),
         ],

time: 287 us -> 249 us (0.87)
  waiting for transfers between devices: 49.3 us -> 0 us
  Pallas kernels: 180 us -> 195 us
  between operations: 22.5 us -> 9.08 us
  local copies, waits for them, and re-layouts: 13.7 us -> 19.8 us
  other arithmetic: 20.7 us -> 24.4 us
    all_gather x1 -> x0, waiting for transfers between devices: 48.6 us -> none  [local(): gathered = lax.all_gather(right_blocks, 'site', axis=1, tiled=True)]
    pallas_call x0 -> x2, Pallas kernels: none -> 27.9 us  [the longest x1 21.1 us: local(): pl.pallas_call(functools.partial(place_kernel, widest, wide, window), gri...]
    pallas_call x1, Pallas kernels: 107 us -> 96 us  [local(): pl.pallas_call(functools.partial(exchange_kernel, groups, sites), out_sha...]
    reshape x0 -> x2, local copies, waits for them, and re-layouts: none -> 5.76 us  [the longest x1 3.76 us: local(): right_blocks.transpose(1, 2, 0, 3).reshape(sec_dev, widest, slots * widest)]
    transpose x1 -> x0, other arithmetic: 3.66 us -> none  [local(): left = left.transpose(1, 0, 2, 3).reshape(sec_dev, slots * widest, widest)]
    select_n x0 -> x1, other arithmetic: none -> 3.53 us  [local(): left = jnp.where(keep, left_blocks, jnp.zeros((), left_blocks.dtype))]
    unnamed x7 -> x11, local copies, waits for them, and re-layouts: 3.98 us -> 6.59 us
  transfers between devices with their start and end apart: 1 -> 0, of which waited for: 1 -> 0; matrix products, arithmetic and copies ran while one was open for 10% -> 0% of each run, Pallas kernels for 0% -> 0%
where the time goes in v2:
time: 249 us
  Pallas kernels  195 us (78%)
  other arithmetic  24.4 us (10%)
  local copies, waits for them, and re-layouts  19.8 us (8%)
  between operations  9.08 us (4%)
    pallas_call x1, Pallas kernels, local(): pl.pallas_call(functools.partial(exchange_kernel, groups, sites), out_sha...  96 us
    pallas_call x1, Pallas kernels, local(): pl.pallas_call(functools.partial(apply_kernel, slots, sec_dev, widest, wi...  71.5 us
    pallas_call x1, Pallas kernels, local(): pl.pallas_call(functools.partial(place_kernel, widest, wide, window), gri...  21.1 us
    pallas_call x1, Pallas kernels, local(): pl.pallas_call(functools.partial(spread_kernel, wide, window), grid=(sect...  6.76 us
    unnamed x11, local copies, waits for them, and re-layouts  6.59 us
    reduce_sum x1, other arithmetic, local(): jnp.sum(vectors_flat.astype(jnp.float32) * diagonal[None], axis=(1, 2))  6.42 us
    lt x8, other arithmetic, local(): jnp.arange(widest, dtype=jnp.int32) < left_size[first_sector + within]  5.02 us

profile of v2, /device:TPU:24, one launch (start us, length us, event | category | flops | bytes accessed | tf_op | source)
XLA Modules:
  0.0 248.7 jit_solution(990889842234190729)
XLA Ops:
  1.3 0.8 convert_reduce_fusion
  2.1 0.7 fusion.4
  10.5 0.6 iota_compare_fusion.6
  11.1 0.6 iota_compare_fusion.10
  11.8 0.6 iota_compare_fusion.5
  12.4 0.6 iota_compare_fusion.9
  13.0 0.6 iota_compare_fusion.4
  13.7 0.6 iota_compare_fusion.8
  14.3 0.6 iota_compare_fusion.7
  14.9 0.6 iota_compare_fusion.11
  15.6 0.8 convert_reduce_fusion.2
  16.4 0.9 pad_dynamic-slice_fusion.7
  17.6 0.7 copy.19.left_e_ref
  18.3 3.5 %and_select_fusion = bf16[8,4,192,192]{3,2,1,0:T(8,128)(2,1)S(1)} fusion(bf16[8,4,192,192]{3,2,1,0:T(8,128)(2,1)} %param.10, pred[4,192]{1,0:T(4,128)(4,1)S(1)} %pad_add_fusion, pred[8,4,192]{2,1,0:T(4,128)(4,1)S(1)} %broadcast_and_fusion), kind=kLoop, calls=%fused_computation.6 | loop fusion | flops 2359296 | bytes 4725504 | tf_op jit(solution)/shard_map/jit(_where)/select_n | solution.py:426
  21.9 2.0 copy.17
  23.8 1.8 copy.18
  25.6 3.8 %reshape.93.right_ref = bf16[4,192,1536]{2,1,0:T(8,128)(2,1)} reshape(bf16[4,192,8,192]{3,2,1,0:T(8,128)(2,1)S(1)} %copy.18) | data formatting | bytes 4718592 | tf_op jit(solution)/shard_map/reshape | solution.py:404
  29.4 3.1 %fusion = (bf16[192,2304]{1,0:T(8,128)(2,1)S(1)}, bf16[192,2304]{1,0:T(8,128)(2,1)S(1)}, bf16[192,2304]{1,0:T(8,128)(2,1)S(1)}, bf16[192,2304]{1,0:T(8,128)(2,1)S(1)}) fusion(s32[]{:T(128)S(6)} %select_n.62, bf16[2048,2048]{1,0:T(8,128)(2,1)} %param.9, pred[192]{0:T(512)(128)(4,1)S(1)} %iota_compare_fusion.7, s32[]{:T(128)S(6)} %select_n.64, ...), kind=kLoop, calls=%fused_computation.8 | loop fusion | flops 1769472 | bytes 11928336 | tf_op jit(solution)/shard_map/jit(_where)/select_n | solution.py:418
  32.6 0.3 pad_maximum_fusion.slab_ref
  32.9 0.4 slice.8
  33.3 0.8 constant_dynamic-slice_fusion.psi_ref
  34.1 3.3 %convert_multiply_fusion = f32[768,2048]{1,0:T(8,128)} fusion(f32[2048]{0:T(1024)S(1)} %copy-done.4, f32[768]{0:T(1024)S(1)} %pad_maximum_fusion.1, bf16[768,2304]{1,0:T(8,128)(2,1)S(1)} %pad_maximum_fusion.slab_ref), kind=kLoop, calls=%fused_computation.5 | loop fusion | flops 4718592 | bytes 9448448 | tf_op jit(solution)/shard_map/mul | solution.py:433
  37.4 6.4 %multiply_reduce_fusion = f32[2]{0:T(128)S(1)} fusion(bf16[2,4,192,2048]{3,2,1,0:T(8,128)(2,1)} %param.17, f32[4,192,2048]{2,1,0:T(8,128)} %bitcast.24), kind=kLoop, calls=%fused_computation | loop fusion | flops 9437182 | bytes 12582920 | tf_op jit(solution)/shard_map/reduce_sum | solution.py:435
  43.9 6.8 %spread_columns.1.spread_ref = bf16[16,768,256]{2,1,0:T(8,128)(2,1)S(1)} custom-call(s32[16]{0:T(128)S(1)} %get-tuple-element.13.starts, s32[16]{0:T(128)S(1)} %get-tuple-element.12.sizes, bf16[768,2304]{1,0:T(8,128)(2,1)S(1)} %pad_maximum_fusion.slab_ref), custom_call_target="tpu_custom_call" | custom-call | tf_op jit(solution)/shard_map/spread_columns/pallas_call | solution.py:442
  50.6 2.6 %copy-done = bf16[16,768,256]{2,1,0:T(8,128)(2,1)} copy-done((bf16[16,768,256]{2,1,0:T(8,128)(2,1)}, bf16[16,768,256]{2,1,0:T(8,128)(2,1)S(1)}, u32[]{:S(2)}) %copy-start) | copy-done | bytes 6291480
  53.2 71.5 %apply_terms.1.added_ref = f32[16,768,256]{2,1,0:T(8,128)} custom-call(bf16[4,2,768,192]{3,2,1,0:T(8,128)(2,1)} %bitcast.26, bf16[16,768,256]{2,1,0:T(8,128)(2,1)} %copy-done, bf16[4,192,1536]{2,1,0:T(8,128)(2,1)} %reshape.93.right_ref), custom_call_target="tpu_custom_call" | custom-call | tf_op jit(solution)/shard_map/apply_terms/pallas_call | solution.py:453
  124.7 21.1 %place_columns.1 = (bf16[768,2048]{1,0:T(8,128)(2,1)}, f32[2,8,128]{2,1,0:T(8,128)}) custom-call(s32[16]{0:T(128)} %copy-done.2, s32[16]{0:T(128)} %copy-done.1, f32[16,768,256]{2,1,0:T(8,128)} %apply_terms.1.added_ref, bf16[2,768,2048]{2,1,0:T(8,128)(2,1)} %bitcast.25), custom_call_target="tpu_custom_call" | custom-call | tf_op jit(solution)/shard_map/place_columns/pallas_call | solution.py:474
  145.9 0.8 reduce_sum.58
  146.7 0.7 broadcast_in_dim.72.corr_ref
  147.3 96.0 %exchange_rows.1 = (bf16[8,96,2048]{2,1,0:T(8,128)(2,1)}, f32[2,8,128]{2,1,0:T(8,128)}) custom-call(bf16[8,96,2048]{2,1,0:T(8,128)(2,1)} %bitcast.29, bf16[96,2048]{1,0:T(8,128)(2,1)} %constant_dynamic-slice_fusion.psi_ref, f32[96,1]{1,0:T(8,128)} %copy.19.left_e_ref, f32[1,2048]{1,0:T(1,128)} %bitcast.31, f32[2,8,128]{2,1,0:T(8,128)} %broadcast_in_dim.72.corr_ref), custom_call_target="tpu_custom_call" | custom-call | tf_op jit(solution)/shard_map/exchange_rows/pallas_call | solution.py:496
  243.4 1.3 slice_reduce_fusion
  244.7 4.0 %copy.22 = bf16[4,192,2048]{2,1,0:T(8,128)(2,1)} copy(bf16[4,192,2048]{2,1,0:T(8,128)(2,1)} %bitcast.30) | data formatting | bytes 6291456
  (15 shorter events, 0.3 us)
Async XLA Ops:
  16.4 27.5 %copy-start.1 = (s32[16]{0:T(128)}, s32[16]{0:T(128)S(1)}, u32[]{:S(2)}) copy-start(s32[16]{0:T(128)S(1)} %get-tuple-element.12.sizes) | copy-start | bytes 196
  16.4 27.5 %copy-start.2 = (s32[16]{0:T(128)}, s32[16]{0:T(128)S(1)}, u32[]{:S(2)}) copy-start(s32[16]{0:T(128)S(1)} %get-tuple-element.13.starts) | copy-start | bytes 196
  18.3 5.5 %copy-start.3 = (bf16[8,4,192,192]{3,2,1,0:T(8,128)(2,1)S(1)}, bf16[8,4,192,192]{3,2,1,0:T(8,128)(2,1)}, u32[]{:S(2)}) copy-start(bf16[8,4,192,192]{3,2,1,0:T(8,128)(2,1)} %param.11) | copy-start | bytes 7077892
  32.5 1.6 copy-start.4
  50.6 2.6 %copy-start = (bf16[16,768,256]{2,1,0:T(8,128)(2,1)}, bf16[16,768,256]{2,1,0:T(8,128)(2,1)S(1)}, u32[]{:S(2)}) copy-start(bf16[16,768,256]{2,1,0:T(8,128)(2,1)S(1)} %spread_columns.1.spread_ref) | copy-start | bytes 18874372
